TPU v7x, 32 devices: a whole 2x2x4 slice. The times are simulated.
32 devices in a mesh: owner: 4 (over y, core), rows: 8 (over z, x).
Axes of the slice: x: 2, y: 2, z: 4, core: 2. Of those that a mesh axis runs over, the one named last changes fastest.
Arguments:
- train_gate: float32 [64, 2048, 1024], P('owner', 'rows'), may hold values from -0.1875 to 0.1875
- other_gate: bfloat16 [64, 2048, 1024], P('owner', 'rows'), may hold values from -0.0625 to 0.0625
- train_up: float32 [64, 2048, 1024], P('owner', 'rows'), may hold values from -0.1875 to 0.1875
- other_up: bfloat16 [64, 2048, 1024], P('owner', 'rows'), may hold values from -0.0625 to 0.0625
- train_down: float32 [64, 1024, 2048], P('owner', None, 'rows'), may hold values from -0.25 to 0.25
- other_down: bfloat16 [64, 1024, 2048], P('owner', None, 'rows'), may hold values from -0.09375 to 0.09375
- router_weight: float32 [2048, 64], P('rows', 'owner'), may hold values from -0.125 to 0.125
- router_gain: float32 [2048], P('rows'), may hold values from 0.25 to 1.75
Outputs:
- ready_gate: bfloat16 [64, 2048, 1024], P('owner', None, 'rows')
- ready_up: bfloat16 [64, 2048, 1024], P('owner', None, 'rows')
- ready_down: bfloat16 [64, 1024, 2048], P('owner', 'rows')
- scale_gate: float32 [64, 1024], P('owner', 'rows')
- scale_up: float32 [64, 1024], P('owner', 'rows')
- scale_down: float32 [64, 1024], P('owner', 'rows')
- serve_router: bfloat16 [2048, 64], replicated
All inputs are finite; a program needn't handle non-finite values. Where the computation divides by a largest or mean magnitude, that divisor is 1e-20 or more.
Results may differ from a plain program's by a relative error of at most 0.001.
Values may be sent and summed in bfloat16 or wider, within the bound.
A program may use at most 192 MiB of HBM per device.

v0:
```python
import jax
import jax.numpy as jnp
from jax import lax
from jax.sharding import PartitionSpec as P


def shards(
    train_gate, other_gate, train_up, other_up, train_down, other_down, router_weight, router_gain
):
    latest_gate = train_gate + other_gate.astype(jnp.float32)
    latest_up = train_up + other_up.astype(jnp.float32)
    latest_down = train_down + other_down.astype(jnp.float32)
    scale_gate, scale_up, scale_down = lax.pmax(
        (
            jnp.max(jnp.abs(latest_gate), axis=1),
            jnp.max(jnp.abs(latest_up), axis=1),
            jnp.max(jnp.abs(latest_down), axis=2),
        ),
        "rows",
    )
    narrow_gate, narrow_up, narrow_down = (
        (latest_gate / jnp.expand_dims(scale_gate, 1)).astype(jnp.bfloat16),
        (latest_up / jnp.expand_dims(scale_up, 1)).astype(jnp.bfloat16),
        (latest_down / jnp.expand_dims(scale_down, 2)).astype(jnp.bfloat16),
    )
    ready_gate, ready_up = (
        lax.all_to_all(narrow_gate, "rows", split_axis=2, concat_axis=1, tiled=True),
        lax.all_to_all(narrow_up, "rows", split_axis=2, concat_axis=1, tiled=True),
    )
    ready_down = lax.all_to_all(narrow_down, "rows", split_axis=1, concat_axis=2, tiled=True)
    scale_gate = lax.dynamic_slice_in_dim(
        scale_gate, lax.axis_index("rows") * ready_gate.shape[2], ready_gate.shape[2], axis=1
    )
    scale_up = lax.dynamic_slice_in_dim(
        scale_up, lax.axis_index("rows") * ready_up.shape[2], ready_up.shape[2], axis=1
    )
    scale_down = lax.dynamic_slice_in_dim(
        scale_down, lax.axis_index("rows") * ready_down.shape[1], ready_down.shape[1], axis=1
    )
    part_router = (router_weight * router_gain[:, None]).astype(jnp.bfloat16)
    row_router = lax.all_gather(part_router, "rows", axis=0, tiled=True)
    serve_router = lax.all_gather(row_router, "owner", axis=1, tiled=True)
    return (ready_gate, ready_up, ready_down, scale_gate, scale_up, scale_down, serve_router)


def solution(mesh):
    placed = (
        P("owner", "rows", None),
        P("owner", "rows", None),
        P("owner", "rows", None),
        P("owner", "rows", None),
        P("owner", None, "rows"),
        P("owner", None, "rows"),
        P("rows", "owner"),
        P("rows"),
    )
    return jax.shard_map(
        shards,
        mesh=mesh,
        in_specs=placed,
        out_specs=(
            P("owner", None, "rows"),
            P("owner", None, "rows"),
            P("owner", "rows", None),
            P("owner", "rows"),
            P("owner", "rows"),
            P("owner", "rows"),
            P(),
        ),
        check_vma=False,
    )
```

profile of v0, /device:TPU:0, one launch (start us, length us, event | category | flops | bytes accessed | tf_op | source)
XLA Modules:
  0.0 877.2 jit_solution(6322543164802641597)
XLA Ops:
  7.2 0.0 all-reduce.3.cloned.1.call-start
  7.2 17.6 %copy.34 = f32[16,256,1024]{1,0,2:T(8,128)} copy(f32[16,256,1024]{2,1,0:T(8,128)} %param.10) | data formatting | bytes 33554432 | tf_op args[2]
  24.8 12.5 %copy.33 = bf16[16,256,1024]{1,0,2:T(8,128)(2,1)} copy(bf16[16,256,1024]{2,1,0:T(8,128)(2,1)} %param.11) | data formatting | bytes 16777216 | tf_op args[3]
  37.3 17.6 %copy.31 = f32[16,256,1024]{1,0,2:T(8,128)} copy(f32[16,256,1024]{2,1,0:T(8,128)} %param.8) | data formatting | bytes 33554432 | tf_op args[0]
  54.9 12.5 %copy.30 = bf16[16,256,1024]{1,0,2:T(8,128)(2,1)} copy(bf16[16,256,1024]{2,1,0:T(8,128)(2,1)} %param.9) | data formatting | bytes 16777216 | tf_op args[1]
  67.4 0.0 copy-start
  67.4 0.0 copy-start.1
  67.4 0.0 slice-start
  67.4 11.1 %abs_reduce_fusion.1 = f32[16,1024]{0,1:T(8,128)} fusion(f32[16,256,1024]{1,0,2:T(8,128)} %copy.34, bf16[16,256,1024]{1,0,2:T(8,128)(2,1)} %copy.33), kind=kLoop, calls=%fused_computation.4 | loop fusion | flops 16760832 | bytes 25231360 | tf_op jit(solution)/shard_map/reduce_max | solution.py:16
  78.5 2.1 copy-done
  80.6 2.4 copy-done.1
  83.0 0.0 slice-start.1
  83.0 4.3 abs_reduce_fusion.2
  87.3 0.0 slice-done
  87.3 0.0 slice-done.1
  87.3 29.3 %abs_reduce_fusion = f32[16,1024]{0,1:T(8,128)} fusion(f32[16,1024,256]{2,1,0:T(8,128)} %param.12, bf16[16,1024,256]{2,1,0:T(8,128)(2,1)S(1)} %bitcast.14), kind=kLoop, calls=%fused_computation.2 | loop fusion | flops 16760832 | bytes 25231360 | tf_op jit(solution)/shard_map/reduce_max | solution.py:17
  116.5 0.0 all-reduce.3.cloned.1.call-update
  116.6 92.5 %all-reduce.3.cloned.1.call-done = (f32[16,1024]{0,1:T(8,128)}, f32[16,1024]{0,1:T(8,128)}, f32[16,1024]{0,1:T(8,128)}) async-done(((f32[16,1024]{0,1:T(8,128)}, f32[16,1024]{0,1:T(8,128)}, f32[16,1024]{0,1:T(8,128)}), (f32[16,1024]{0,1:T(8,128)}, f32[16,1024]{0,1:T(8,128)}, f32[16,1024]{0,1:T(8,128)})) %all-reduce.3.cloned.1.call-update) | async-done | bytes 196624 | tf_op jit(solution)/shard_map/pmax | solution.py:13
  209.0 20.5 %divide_convert_fusion.1 = (bf16[16,256,1024]{1,0,2:T(8,128)(2,1)}, bf16[16,256,1024]{1,0,2:T(8,128)(2,1)S(1)}) fusion(f32[16,256,1024]{1,0,2:T(8,128)} %copy.34, bf16[16,256,1024]{1,0,2:T(8,128)(2,1)} %copy.33, f32[16,1024]{0,1:T(8,128)} %get-tuple-element.15, f32[16,1024]{0,1:T(8,128)} %get-tuple-element.14, f32[16,256,1024]{1,0,2:T(8,128)} %copy.31, ...), kind=kLoop, calls=%fused_computation.3 | loop fusion | flops 33554432 | bytes 67239936 | tf_op jit(solution)/shard_map/convert_element_type | solution.py:23
  229.6 0.0 copy-start.2
  229.6 187.0 %all_to_all.54 = bf16[16,256,1024]{1,0,2:T(8,128)(2,1)} all-to-all(bf16[16,256,1024]{1,0,2:T(8,128)(2,1)S(1)} %get-tuple-element.18), channel_id=1, replica_groups=mesh['owner'=4,'rows'=8] {'rows'}, dimensions={2} | all-to-all | bytes 16777216 | tf_op jit(solution)/shard_map/all_to_all | solution.py:27
  416.6 4.9 all-to-all-start.1
  421.5 0.0 copy-done.2
  421.5 23.8 %divide_convert_fusion = bf16[16,1024,256]{2,0,1:T(8,128)(2,1)} fusion(f32[16,1024,256]{2,1,0:T(8,128)} %param.12, f32[16,1024]{0,1:T(8,128)S(1)} %copy-done.2, bf16[16,1024,256]{2,1,0:T(8,128)(2,1)} %param.13), kind=kLoop, calls=%fused_computation.1 | loop fusion | flops 16777216 | bytes 33619968 | tf_op jit(solution)/shard_map/convert_element_type | solution.py:24
  445.3 0.0 copy-start.3
  445.3 0.0 copy-start.4
  445.3 158.3 %all-to-all-done.1 = bf16[16,256,1024]{1,0,2:T(8,128)(2,1)} async-done(((bf16[16,256,1024]{1,0,2:T(8,128)(2,1)}), bf16[16,256,1024]{1,0,2:T(8,128)(2,1)}, u32[]{:S(2)}, u32[]{:S(2)}) %all-to-all-start.1) | async-done | bytes 8388640 | tf_op jit(solution)/shard_map/all_to_all | solution.py:28
  603.6 5.0 all-to-all-start.2
  608.6 0.0 copy-done.3
  608.7 0.0 copy-done.4
  608.7 201.9 %all_gather.6 = bf16[2048,16]{0,1:T(8,128)(2,1)S(1)} all-gather(bf16[256,16]{0,1:T(8,128)(2,1)S(1)} %multiply_convert_fusion), channel_id=1, replica_groups=mesh['owner'=4,'rows'=8] {'rows'}, dimensions={0}, use_global_device_ids=true | all-gather | bytes 73728 | tf_op jit(solution)/shard_map/all_gather | solution.py:41
  810.6 6.0 all_gather.7
  816.5 0.8 constant_dynamic-slice_fusion
  817.4 0.7 copy.40
  818.1 0.7 copy.41
  818.7 0.8 constant_dynamic-slice_fusion.2
  819.6 0.7 copy.39
  820.2 12.3 %copy.32 = bf16[16,8,256,128]{3,2,1,0:T(8,128)(2,1)} copy(bf16[16,8,256,128]{2,0,3,1:T(8,128)(2,1)} %bitcast.15) | data formatting | bytes 16777216 | tf_op jit(solution)/shard_map/all_to_all | solution.py:27
  832.5 12.3 %copy.35 = bf16[16,8,256,128]{3,2,1,0:T(8,128)(2,1)} copy(bf16[16,8,256,128]{2,0,3,1:T(8,128)(2,1)} %bitcast.4) | data formatting | bytes 16777216 | tf_op jit(solution)/shard_map/all_to_all | solution.py:28
  844.8 0.0 all-to-all-done.2
  844.8 11.4 %copy.38 = bf16[16,128,8,256]{3,2,1,0:T(8,128)(2,1)} copy(bf16[16,128,8,256]{3,0,1,2:T(8,128)(2,1)} %bitcast.7) | data formatting | bytes 16777216 | tf_op jit(solution)/shard_map/all_to_all | solution.py:30
  856.2 13.4 %all_to_all.50 = bf16[16,128,2048]{2,1,0:T(8,128)(2,1)} reshape(bf16[16,128,8,256]{3,2,1,0:T(8,128)(2,1)} %copy.38) | data formatting | bytes 16777216 | tf_op jit(solution)/shard_map/all_to_all | solution.py:30
  869.6 0.7 copy.53
  (2 shorter events, 0.0 us)
Async XLA Ops:
  7.2 201.9 %all-reduce.3.cloned.1.call-start = ((), (), s32[]{:S(2)}) async-start(), calls=%async_computation.3 | async-start | bytes 3145728 | tf_op jit(solution)/shard_map/pmax | solution.py:13
  67.4 13.2 %copy-start = (f32[16,256,1024]{1,0,2:T(8,128)S(1)}, f32[16,256,1024]{1,0,2:T(8,128)}, u32[]{:S(2)}) copy-start(f32[16,256,1024]{1,0,2:T(8,128)} %copy.31) | copy-start | bytes 50331652
  67.4 15.6 %copy-start.1 = (bf16[16,256,1024]{1,0,2:T(8,128)(2,1)S(1)}, bf16[16,256,1024]{1,0,2:T(8,128)(2,1)}, u32[]{:S(2)}) copy-start(bf16[16,256,1024]{1,0,2:T(8,128)(2,1)} %copy.30) | copy-start | bytes 25165828
  67.4 19.9 %slice-start = ((s8[8388608]{0:T(1024)(128)(4,1)}), s8[4194304]{0:T(1024)(128)(4,1)S(1)}, s32[]{:S(2)}) async-start(s8[8388608]{0:T(1024)(128)(4,1)} %bitcast.13), calls=%async_computation.4 | async-start | bytes 8388608
  83.0 4.3 slice-start.1
  229.6 192.0 %copy-start.2 = (f32[16,1024]{0,1:T(8,128)S(1)}, f32[16,1024]{0,1:T(8,128)}, u32[]{:S(2)}) copy-start(f32[16,1024]{0,1:T(8,128)} %get-tuple-element.16) | copy-start | bytes 196612
  416.6 187.0 %all-to-all-start.1 = ((bf16[16,256,1024]{1,0,2:T(8,128)(2,1)}), bf16[16,256,1024]{1,0,2:T(8,128)(2,1)}, u32[]{:S(2)}, u32[]{:S(2)}) async-start(bf16[16,256,1024]{1,0,2:T(8,128)(2,1)} %get-tuple-element.17), calls=%async_computation.1 | async-start | bytes 16777216 | tf_op jit(solution)/shard_map/all_to_all | solution.py:28
  445.3 163.3 %copy-start.3 = (f32[256,16]{0,1:T(8,128)S(1)}, f32[256,16]{0,1:T(8,128)}, u32[]{:S(2)}) copy-start(f32[256,16]{0,1:T(8,128)} %param.14) | copy-start | bytes 49156
  445.3 163.3 %copy-start.4 = (f32[256]{0:T(256)S(1)}, f32[256]{0:T(256)}, u32[]{:S(2)}) copy-start(f32[256]{0:T(256)} %param.15) | copy-start | bytes 3076
  603.6 241.2 %all-to-all-start.2 = ((bf16[16,1024,256]{2,0,1:T(8,128)(2,1)}), bf16[16,1024,256]{2,0,1:T(8,128)(2,1)}, u32[]{:S(2)}, u32[]{:S(2)}) async-start(bf16[16,1024,256]{2,0,1:T(8,128)(2,1)} %divide_convert_fusion), calls=%async_computation.2 | async-start | bytes 16777216 | tf_op jit(solution)/shard_map/all_to_all | solution.py:30
Sparse Core Ops, SparseCore 0:
  116.7 92.2 all-reduce.2
where the time goes:
time: 880 us; the launch traced here: 877 us
  blocking collectives  395 us (45%)
  waiting for transfers between devices  251 us (29%)
  local copies, waits for them, and re-layouts  118 us (13%)
  other arithmetic  88.9 us (10%)
  between operations  14.1 us (2%)
  starting transfers between devices  10 us (1%)
    all_gather x1, blocking collectives, shards(): row_router = lax.all_gather(part_router, 'rows', axis=0, tiled=True)  202 us
    all_to_all x1, blocking collectives, shards(): lax.all_to_all(narrow_gate, 'rows', split_axis=2, concat_axis=1, tiled=True)  187 us
    all_to_all x1, waiting for transfers between devices, shards(): lax.all_to_all(narrow_up, 'rows', split_axis=2, concat_axis=1, tiled=True)  158 us
    pmax x1, waiting for transfers between devices, shards(): lax.pmax((jnp.max(jnp.abs(latest_gate), axis=1), jnp.max(jnp.abs(latest_u...  92.5 us
    unnamed x22, local copies, waits for them, and re-layouts  67.4 us
    reduce_max x1, other arithmetic, shards(): jnp.max(jnp.abs(latest_down), axis=2)  29.3 us
    all_to_all x2, local copies, waits for them, and re-layouts, shards(): lax.all_to_all(narrow_down, 'rows', split_axis=1, concat_axis=2, tiled=True)  24.8 us
    convert_element_type x1, other arithmetic, shards(): (latest_down / jnp.expand_dims(scale_down, 2)).astype(jnp.bfloat16)  23.8 us
  transfers between devices with their start and end apart: 3, of which 2 were waited for; matrix products, arithmetic and copies ran while one was open for 6% of the time, Pallas kernels for 0%

commit v1 on v0

--- a/solution.py
+++ b/solution.py
@@ -25,7 +25,12 @@
     )
     ready_gate, ready_up = (
         lax.all_to_all(narrow_gate, "rows", split_axis=2, concat_axis=1, tiled=True),
-        lax.all_to_all(narrow_up, "rows", split_axis=2, concat_axis=1, tiled=True),
+        jnp.concatenate(
+            lax.all_to_all(
+                jnp.stack(jnp.split(narrow_up, lax.axis_size("rows"), axis=2)), "rows", 0, 0
+            ),
+            axis=1,
+        ),
     )
     ready_down = lax.all_to_all(narrow_down, "rows", split_axis=1, concat_axis=2, tiled=True)
     scale_gate = lax.dynamic_slice_in_dim(

time: 880 us -> 822 us (0.934)
  blocking collectives: 395 us -> 208 us
  waiting for transfers between devices: 251 us -> 404 us
  local copies, waits for them, and re-layouts: 118 us -> 88.5 us
    all_to_all x1 -> x0, blocking collectives: 187 us -> none  [shards(): lax.all_to_all(narrow_gate, 'rows', split_axis=2, concat_axis=1, tiled=True)]
    all_to_all x1 -> x2, waiting for transfers between devices: 158 us -> 321 us  [the longest x1 163 us: shards(): lax.all_to_all(narrow_gate, 'rows', split_axis=2, concat_axis=1, tiled=True)]
    unnamed x22 -> x28, local copies, waits for them, and re-layouts: 67.4 us -> 40.9 us
    all_to_all x1 -> x0, local copies, waits for them, and re-layouts: 12.3 us -> none  [shards(): lax.all_to_all(narrow_up, 'rows', split_axis=2, concat_axis=1, tiled=True)]
    convert_element_type x0 -> x1, other arithmetic: none -> 12.1 us  [shards(): (latest_gate / jnp.expand_dims(scale_gate, 1)).astype(jnp.bfloat16)]
    convert_element_type x1, other arithmetic: 20.5 us -> 9.39 us  [shards(): (latest_up / jnp.expand_dims(scale_up, 1)).astype(jnp.bfloat16)]
    pmax x1, waiting for transfers between devices: 92.5 us -> 82.4 us  [shards(): lax.pmax((jnp.max(jnp.abs(latest_gate), axis=1), jnp.max(jnp.abs(latest_u...]
  transfers between devices with their start and end apart: 3 -> 4, of which waited for: 2 -> 3; matrix products, arithmetic and copies ran while one was open for 6% -> 8% of each run, Pallas kernels for 0% -> 0%
where the time goes in v1:
time: 822 us; the launch traced here: 820 us
  waiting for transfers between devices  404 us (49%)
  blocking collectives  208 us (25%)
  other arithmetic  90.5 us (11%)
  local copies, waits for them, and re-layouts  88.5 us (11%)
  starting transfers between devices  15.3 us (2%)
  between operations  14.1 us (2%)
    all_gather x1, blocking collectives, shards(): row_router = lax.all_gather(part_router, 'rows', axis=0, tiled=True)  202 us
    all_to_all x1, waiting for transfers between devices, shards(): lax.all_to_all(narrow_gate, 'rows', split_axis=2, concat_axis=1, tiled=True)  163 us
    all_to_all x1, waiting for transfers between devices, shards(): lax.all_to_all(jnp.stack(jnp.split(narrow_up, lax.axis_size('rows'), axis...  158 us
    pmax x1, waiting for transfers between devices, shards(): lax.pmax((jnp.max(jnp.abs(latest_gate), axis=1), jnp.max(jnp.abs(latest_u...  82.4 us
    unnamed x28, local copies, waits for them, and re-layouts  40.9 us
    all_to_all x2, local copies, waits for them, and re-layouts, shards(): lax.all_to_all(narrow_down, 'rows', split_axis=1, concat_axis=2, tiled=True)  24.8 us
    reduce_max x1, other arithmetic, shards(): jnp.max(jnp.abs(latest_down), axis=2)  24.4 us
    convert_element_type x1, other arithmetic, shards(): (latest_down / jnp.expand_dims(scale_down, 2)).astype(jnp.bfloat16)  23.8 us
  transfers between devices with their start and end apart: 4, of which 3 were waited for; matrix products, arithmetic and copies ran while one was open for 8% of the time, Pallas kernels for 0%

profile of v1, /device:TPU:0, one launch (start us, length us, event | category | flops | bytes accessed | tf_op | source)
XLA Modules:
  0.0 820.4 jit_solution(3453497732132076611)
XLA Ops:
  7.2 0.0 all-reduce.3.cloned.1.call-start
  7.2 17.6 %copy.28 = f32[16,256,1024]{1,0,2:T(8,128)} copy(f32[16,256,1024]{2,1,0:T(8,128)} %param.8) | data formatting | bytes 33554432 | tf_op args[0]
  24.8 12.5 %copy.27 = bf16[16,256,1024]{1,0,2:T(8,128)(2,1)} copy(bf16[16,256,1024]{2,1,0:T(8,128)(2,1)} %param.9) | data formatting | bytes 16777216 | tf_op args[1]
  37.3 0.0 slice-start
  37.3 0.0 slice-start.1
  37.3 0.0 slice-start.2
  37.3 11.1 %abs_reduce_fusion.2 = f32[16,1024]{0,1:T(8,128)} fusion(f32[16,256,1024]{1,0,2:T(8,128)} %copy.28, bf16[16,256,1024]{1,0,2:T(8,128)(2,1)} %copy.27), kind=kLoop, calls=%fused_computation.7 | loop fusion | flops 16760832 | bytes 25231360 | tf_op jit(solution)/shard_map/reduce_max | solution.py:15
  48.4 0.0 slice-start.3
  48.4 9.8 %abs_reduce_fusion.1 = f32[16,1024]{1,0:T(8,128)} fusion(f32[16,256,1024]{2,1,0:T(8,128)} %param.10, bf16[16,256,1024]{2,1,0:T(8,128)(2,1)} %param.11), kind=kLoop, calls=%fused_computation.4 | loop fusion | flops 16760832 | bytes 25231360 | tf_op jit(solution)/shard_map/reduce_max | solution.py:16
  58.2 0.0 slice-done
  58.2 0.0 slice-done.1
  58.2 0.0 slice-done.2
  58.2 0.0 slice-done.3
  58.2 24.4 %abs_reduce_fusion = f32[16,1024]{0,1:T(8,128)} fusion(f32[16,1024,256]{2,1,0:T(8,128)S(1)} %bitcast.44, bf16[16,1024,256]{2,1,0:T(8,128)(2,1)} %param.13), kind=kLoop, calls=%fused_computation.2 | loop fusion | flops 16760832 | bytes 25231360 | tf_op jit(solution)/shard_map/reduce_max | solution.py:17
  82.6 0.0 all-reduce.3.cloned.1.call-update
  82.6 82.4 %all-reduce.3.cloned.1.call-done = (f32[16,1024]{0,1:T(8,128)}, f32[16,1024]{1,0:T(8,128)}, f32[16,1024]{0,1:T(8,128)}) async-done(((f32[16,1024]{0,1:T(8,128)}, f32[16,1024]{1,0:T(8,128)}, f32[16,1024]{0,1:T(8,128)}), (f32[16,1024]{0,1:T(8,128)}, f32[16,1024]{1,0:T(8,128)}, f32[16,1024]{0,1:T(8,128)})) %all-reduce.3.cloned.1.call-update) | async-done | bytes 196624 | tf_op jit(solution)/shard_map/pmax | solution.py:13
  165.0 12.1 %divide_convert_fusion.2 = bf16[16,256,1024]{1,0,2:T(8,128)(2,1)} fusion(f32[16,256,1024]{1,0,2:T(8,128)} %copy.28, bf16[16,256,1024]{1,0,2:T(8,128)(2,1)} %copy.27, f32[16,1024]{0,1:T(8,128)} %get-tuple-element.14), kind=kLoop, calls=%fused_computation.6 | loop fusion | flops 16777216 | bytes 33619968 | tf_op jit(solution)/shard_map/convert_element_type | solution.py:22
  177.1 0.0 copy-start.1
  177.1 5.3 all-to-all-start
  182.3 0.0 copy-done.1
  182.3 9.4 %divide_convert_fusion.1 = bf16[16,256,1024]{2,1,0:T(8,128)(2,1)S(1)} fusion(f32[16,256,1024]{2,1,0:T(8,128)} %param.10, bf16[16,256,1024]{2,1,0:T(8,128)(2,1)} %param.11, f32[16,1024]{1,0:T(8,128)S(1)} %copy-done.1), kind=kLoop, calls=%fused_computation.3 | loop fusion | flops 16777216 | bytes 33619968 | tf_op jit(solution)/shard_map/convert_element_type | solution.py:23
  191.7 1.2 fusion.7
  193.0 1.2 fusion.6
  194.2 1.2 fusion.5
  195.5 1.2 fusion.4
  196.7 1.2 fusion.3
  198.0 1.2 fusion.2
  199.2 1.2 fusion.1
  200.5 1.2 fusion
  201.7 0.0 copy-start
  201.7 163.3 %all-to-all-done = bf16[16,256,1024]{1,0,2:T(8,128)(2,1)} async-done(((bf16[16,256,1024]{1,0,2:T(8,128)(2,1)}), bf16[16,256,1024]{1,0,2:T(8,128)(2,1)}, u32[]{:S(2)}, u32[]{:S(2)}) %all-to-all-start) | async-done | bytes 8388640 | tf_op jit(solution)/shard_map/all_to_all | solution.py:27
  365.0 5.0 all-to-all-start.1
  370.0 0.0 copy-done
  370.0 23.8 %divide_convert_fusion = bf16[16,1024,256]{2,0,1:T(8,128)(2,1)} fusion(f32[16,1024,256]{2,1,0:T(8,128)} %param.12, f32[16,1024]{0,1:T(8,128)S(1)} %copy-done, bf16[16,1024,256]{2,1,0:T(8,128)(2,1)} %param.13), kind=kLoop, calls=%fused_computation.1 | loop fusion | flops 16777216 | bytes 33619968 | tf_op jit(solution)/shard_map/convert_element_type | solution.py:24
  393.8 0.0 copy-start.2
  393.8 0.0 copy-start.3
  393.8 158.2 %all-to-all-done.1 = bf16[8,16,256,128]{3,2,1,0:T(8,128)(2,1)} async-done(((bf16[8,16,256,128]{3,2,1,0:T(8,128)(2,1)}), bf16[8,16,256,128]{3,2,1,0:T(8,128)(2,1)}, u32[]{:S(2)}, u32[]{:S(2)}) %all-to-all-start.1) | async-done | bytes 8388640 | tf_op jit(solution)/shard_map/all_to_all | solution.py:29
  552.0 5.0 all-to-all-start.2
  557.0 0.0 copy-done.2
  557.0 0.0 copy-done.3
  557.0 202.1 %all_gather.6 = bf16[2048,16]{0,1:T(8,128)(2,1)S(1)} all-gather(bf16[256,16]{0,1:T(8,128)(2,1)S(1)} %multiply_convert_fusion), channel_id=1, replica_groups=mesh['owner'=4,'rows'=8] {'rows'}, dimensions={0}, use_global_device_ids=true | all-gather | bytes 73728 | tf_op jit(solution)/shard_map/all_gather | solution.py:46
  759.1 6.0 all_gather.7
  765.1 0.8 constant_dynamic-slice_fusion
  766.0 0.7 copy.34
  766.6 0.7 copy.35
  767.3 0.6 constant_dynamic-slice_fusion.1
  767.9 12.3 %copy.29 = bf16[16,8,256,128]{3,2,1,0:T(8,128)(2,1)} copy(bf16[16,8,256,128]{2,0,3,1:T(8,128)(2,1)} %bitcast.1) | data formatting | bytes 16777216 | tf_op jit(solution)/shard_map/all_to_all | solution.py:27
  780.2 7.9 copy.30
  788.1 0.0 all-to-all-done.2
  788.1 11.4 %copy.33 = bf16[16,128,8,256]{3,2,1,0:T(8,128)(2,1)} copy(bf16[16,128,8,256]{3,0,1,2:T(8,128)(2,1)} %bitcast.14) | data formatting | bytes 16777216 | tf_op jit(solution)/shard_map/all_to_all | solution.py:35
  799.4 13.4 %all_to_all.37 = bf16[16,128,2048]{2,1,0:T(8,128)(2,1)} reshape(bf16[16,128,8,256]{3,2,1,0:T(8,128)(2,1)} %copy.33) | data formatting | bytes 16777216 | tf_op jit(solution)/shard_map/all_to_all | solution.py:35
  812.9 0.7 copy.54
  (2 shorter events, 0.0 us)
Async XLA Ops:
  7.2 157.8 %all-reduce.3.cloned.1.call-start = ((), (), s32[]{:S(2)}) async-start(), calls=%async_computation.3 | async-start | bytes 2228224 | tf_op jit(solution)/shard_map/pmax | solution.py:13
  37.3 20.9 %slice-start = ((s8[16777216]{0:T(1024)(128)(4,1)}), s8[4194304]{0:T(1024)(128)(4,1)S(1)}, s32[]{:S(2)}) async-start(s8[16777216]{0:T(1024)(128)(4,1)} %bitcast.43), calls=%async_computation.4 | async-start | bytes 8388608
  37.3 20.9 %slice-start.1 = ((s8[16777216]{0:T(1024)(128)(4,1)}), s8[4194304]{0:T(1024)(128)(4,1)S(1)}, s32[]{:S(2)}) async-start(s8[16777216]{0:T(1024)(128)(4,1)} %bitcast.43), calls=%async_computation.5 | async-start | bytes 8388608
  37.3 20.9 %slice-start.2 = ((s8[16777216]{0:T(1024)(128)(4,1)}), s8[4194304]{0:T(1024)(128)(4,1)S(1)}, s32[]{:S(2)}) async-start(s8[16777216]{0:T(1024)(128)(4,1)} %bitcast.43), calls=%async_computation.6 | async-start | bytes 8388608
  48.4 9.8 %slice-start.3 = ((s8[16777216]{0:T(1024)(128)(4,1)}), s8[4194304]{0:T(1024)(128)(4,1)S(1)}, s32[]{:S(2)}) async-start(s8[16777216]{0:T(1024)(128)(4,1)} %bitcast.43), calls=%async_computation.7 | async-start | bytes 8388608
  177.1 5.3 copy-start.1
  177.1 187.9 %all-to-all-start = ((bf16[16,256,1024]{1,0,2:T(8,128)(2,1)}), bf16[16,256,1024]{1,0,2:T(8,128)(2,1)}, u32[]{:S(2)}, u32[]{:S(2)}) async-start(bf16[16,256,1024]{1,0,2:T(8,128)(2,1)} %divide_convert_fusion.2), calls=%async_computation | async-start | bytes 16777216 | tf_op jit(solution)/shard_map/all_to_all | solution.py:27
  201.7 168.3 %copy-start = (f32[16,1024]{0,1:T(8,128)S(1)}, f32[16,1024]{0,1:T(8,128)}, u32[]{:S(2)}) copy-start(f32[16,1024]{0,1:T(8,128)} %get-tuple-element.16) | copy-start | bytes 196612
  365.0 187.1 %all-to-all-start.1 = ((bf16[8,16,256,128]{3,2,1,0:T(8,128)(2,1)}), bf16[8,16,256,128]{3,2,1,0:T(8,128)(2,1)}, u32[]{:S(2)}, u32[]{:S(2)}) async-start(bf16[8,16,256,128]{3,2,1,0:T(8,128)(2,1)} %fusion), calls=%async_computation.1 | async-start | bytes 16777216 | tf_op jit(solution)/shard_map/all_to_all | solution.py:29
  393.8 163.2 %copy-start.2 = (f32[256,16]{0,1:T(8,128)S(1)}, f32[256,16]{0,1:T(8,128)}, u32[]{:S(2)}) copy-start(f32[256,16]{0,1:T(8,128)} %param.14) | copy-start | bytes 49156
  393.8 163.2 %copy-start.3 = (f32[256]{0:T(256)S(1)}, f32[256]{0:T(256)}, u32[]{:S(2)}) copy-start(f32[256]{0:T(256)} %param.15) | copy-start | bytes 3076
  552.0 236.0 %all-to-all-start.2 = ((bf16[16,1024,256]{2,0,1:T(8,128)(2,1)}), bf16[16,1024,256]{2,0,1:T(8,128)(2,1)}, u32[]{:S(2)}, u32[]{:S(2)}) async-start(bf16[16,1024,256]{2,0,1:T(8,128)(2,1)} %divide_convert_fusion), calls=%async_computation.2 | async-start | bytes 16777216 | tf_op jit(solution)/shard_map/all_to_all | solution.py:35
Sparse Core Ops, SparseCore 0:
  82.7 82.2 all-reduce.2
